TPU v7x, 32 devices: a whole 2x2x4 slice. The times are simulated.
32 devices in a mesh: copy: 2 (over core), fsdp: 4 (over z), tp: 4 (over y, x).
Axes of the slice: x: 2, y: 2, z: 4, core: 2. Of those that a mesh axis runs over, the one named last changes fastest.
Arguments:
- gradients: float32 [32, 128, 4096], P('copy', 'fsdp', 'tp'), parts along dimension 0, may hold values from -6 to 6
- momentum: float32 [32, 128, 4096], P('copy', 'fsdp', 'tp'), parts along dimension 0, may hold values from -6 to 6
- weights: float32 [32, 128, 4096], P('copy', 'fsdp', 'tp'), parts along dimension 0, may hold values from -0.1875 to 0.1875
Outputs:
- new_weights: float32 [32, 128, 4096], P('copy', 'fsdp', 'tp'), parts along dimension 0
- new_momentum: float32 [32, 128, 4096], P('copy', 'fsdp', 'tp'), parts along dimension 0
There are 2 independent parts, one for each index of `copy`. A program takes and returns all parts, laid end to end along the dimension named above; each array names one. Nothing has to cross between parts.
All inputs are finite; a program needn't handle non-finite values.
Results may differ from a plain program's by a relative error of at most 0.00014.
Values sent between devices are 32-bit elements; how exact they have to be, the bound alone decides.
A program may use at most 64 MiB of HBM per device.

v0:
```python
import jax
import jax.numpy as jnp
from jax import lax
from jax.sharding import PartitionSpec as P

ITERS = 4
hold_rate = 0.95
learn_rate = 0.9
decay_rate = 0.1


def mul(a, b):
    return jnp.einsum("mij,mjk->mik", a, b, precision=lax.Precision.HIGHEST)


def mixing(gram):
    eye = jnp.eye(gram.shape[-1], dtype=gram.dtype)
    scale = lax.rsqrt(jnp.sum(gram * eye, axis=(1, 2), keepdims=True) + 1e-06)
    gram = gram * scale * scale
    total = scale * eye
    for step in range(ITERS):
        poly = 3.4445 * eye - 4.775 * gram + 2.0315 * mul(gram, gram)
        total = mul(poly, total)
        if step < ITERS - 1:
            gram = mul(poly, mul(gram, poly))
    return total


def shards(gradients, momentum, weights):
    new_momentum = hold_rate * momentum + gradients
    direction = hold_rate * new_momentum + gradients
    moved = lax.all_to_all(direction, "fsdp", split_axis=0, concat_axis=1, tiled=True)
    gram = jnp.einsum("mik,mjk->mij", moved, moved, precision=lax.Precision.HIGHEST)
    gram = lax.psum(gram, "tp")
    iterate = mul(mixing(gram), moved)
    back = lax.all_to_all(iterate, "fsdp", split_axis=1, concat_axis=0, tiled=True)
    new_weights = (1.0 - learn_rate * decay_rate) * weights - learn_rate * back
    return (new_weights, new_momentum)


def solution(mesh):
    return jax.shard_map(
        shards,
        mesh=mesh,
        in_specs=(P("copy", "fsdp", "tp"), P("copy", "fsdp", "tp"), P("copy", "fsdp", "tp")),
        out_specs=(P("copy", "fsdp", "tp"), P("copy", "fsdp", "tp")),
        check_vma=False,
    )
```

profile of v0, /device:TPU:0, one launch (start us, length us, event | category | flops | bytes accessed | tf_op | source)
XLA Modules:
  0.0 186.5 jit_solution(14155956798188366832)
XLA Ops:
  7.2 0.0 all-reduce.2.cloned.1.call-start
  7.2 4.5 %multiply_add_fusion = (f32[16,32,1024]{2,1,0:T(8,128)S(1)}, f32[16,32,1024]{2,1,0:T(8,128)}) fusion(f32[16,32,1024]{2,1,0:T(8,128)} %param.3, f32[16,32,1024]{2,1,0:T(8,128)} %param.4), kind=kLoop, calls=%fused_computation.1 | loop fusion | flops 2097152 | bytes 8388608 | tf_op jit(solution)/shard_map/add | solution.py:31
  11.7 54.3 %all_to_all.27 = f32[16,32,1024]{2,1,0:T(8,128)S(1)} all-to-all(f32[16,32,1024]{2,1,0:T(8,128)S(1)} %get-tuple-element.2), channel_id=1, replica_groups=mesh['copy'=2,'fsdp'=4,'tp'=4] {'fsdp'}, dimensions={0} | all-to-all | bytes 4194304 | tf_op jit(solution)/shard_map/all_to_all | solution.py:32
  66.0 0.1 copy.7
  66.2 2.8 %fusion.13 = f32[4,128,128]{2,1,0:T(8,128)} fusion(f32[4,128,1024]{2,1,0:T(8,128)S(1)} %bitcast.37), kind=kOutput, calls=%fused_computation.25 | convolution fusion | flops 805306368 | bytes 2359296 | tf_op jit(solution)/shard_map/mik,mjk->mij/dot_general | solution.py:33
  68.9 0.0 all-reduce.2.cloned.1.call-update
  69.0 42.4 %all-reduce.2.cloned.1.call-done = f32[4,128,128]{2,1,0:T(8,128)} async-done(((f32[4,128,128]{2,1,0:T(8,128)}), f32[4,128,128]{2,1,0:T(8,128)}) %all-reduce.2.cloned.1.call-update) | async-done | bytes 262160 | tf_op jit(solution)/shard_map/psum | solution.py:34
  111.4 1.1 multiply_reduce_fusion
  112.5 1.6 fusion.3
  114.1 0.4 fusion.4
  114.6 1.4 fusion.6
  116.0 0.4 fusion.14
  116.4 0.4 fusion.2
  116.7 0.4 fusion.15
  117.1 0.4 fusion.19
  117.5 0.4 fusion.16
  118.0 0.4 fusion.1
  118.3 0.4 fusion.17
  118.7 0.4 fusion.20
  119.1 0.4 fusion.18
  119.5 0.4 fusion
  119.9 0.4 fusion.21
  120.3 1.9 %fusion.22 = f32[4,128,1024]{2,1,0:T(8,128)S(1)} fusion(f32[4,128,128]{2,1,0:T(8,128)S(1)} %fusion.21, f32[4,128,1024]{2,1,0:T(8,128)S(1)} %bitcast.38), kind=kOutput, calls=%fused_computation.34 | convolution fusion | flops 805306368 | bytes 4456448 | tf_op jit(solution)/shard_map/mij,mjk->mik/dot_general | solution.py:13
  122.3 1.4 copy.8
  123.6 52.1 %all_to_all.28 = f32[4,128,1024]{2,0,1:T(4,128)S(1)} all-to-all(f32[4,128,1024]{2,0,1:T(4,128)S(1)} %copy.8), channel_id=1, replica_groups=mesh['copy'=2,'fsdp'=4,'tp'=4] {'fsdp'}, dimensions={1} | all-to-all | bytes 4194304 | tf_op jit(solution)/shard_map/all_to_all | solution.py:36
  175.7 0.6 broadcast_multiply_fusion
  176.3 0.0 copy-start
  176.3 1.2 copy.9
  177.6 0.4 copy-done
  177.9 1.8 bitcast_subtract_fusion
  (3 shorter events, 0.0 us)
Async XLA Ops:
  7.2 104.2 %all-reduce.2.cloned.1.call-start = ((), (), s32[]{:S(2)}) async-start(), calls=%async_computation.2 | async-start | bytes 524288 | tf_op jit(solution)/shard_map/psum | solution.py:34
  176.3 1.6 copy-start
Sparse Core Ops, SparseCore 0:
  69.1 42.2 all-reduce.1
where the time goes:
time: 187 us
  blocking collectives  106 us (57%)
  waiting for transfers between devices  42.4 us (23%)
  between operations  14.2 us (8%)
  matrix products  12.4 us (7%)
  other arithmetic  7.95 us (4%)
  local copies, waits for them, and re-layouts  3.07 us (2%)
    all_to_all x1, blocking collectives, shards(): lax.all_to_all(direction, 'fsdp', split_axis=0, concat_axis=1, tiled=True)  54.3 us
    all_to_all x1, blocking collectives, shards(): lax.all_to_all(iterate, 'fsdp', split_axis=1, concat_axis=0, tiled=True)  52.1 us
    psum x1, waiting for transfers between devices, shards(): gram = lax.psum(gram, 'tp')  42.4 us
    dot_general x15, matrix products, mul(): return jnp.einsum('mij,mjk->mik', a, b, precision=lax.Precision.HIGHEST)  9.65 us
    add x1, other arithmetic, shards(): direction = hold_rate * new_momentum + gradients  4.5 us
  transfers between devices with their start and end apart: 1, of which 1 were waited for; matrix products, arithmetic and copies ran while one was open for 0% of the time, Pallas kernels for 0%

commit v1 on v0

--- a/solution.py
+++ b/solution.py
@@ -31,7 +31,7 @@
     direction = hold_rate * new_momentum + gradients
     moved = lax.all_to_all(direction, "fsdp", split_axis=0, concat_axis=1, tiled=True)
     gram = jnp.einsum("mik,mjk->mij", moved, moved, precision=lax.Precision.HIGHEST)
-    gram = lax.psum(gram, "tp")
+    gram = jnp.sum(lax.all_gather(gram, "tp"), axis=0)
     iterate = mul(mixing(gram), moved)
     back = lax.all_to_all(iterate, "fsdp", split_axis=1, concat_axis=0, tiled=True)
     new_weights = (1.0 - learn_rate * decay_rate) * weights - learn_rate * back

time: 187 us -> 169 us (0.904)
  waiting for transfers between devices: 42.4 us -> 25.9 us
  matrix products: 12.4 us -> 10.3 us
    psum x1 -> x0, waiting for transfers between devices: 42.4 us -> none  [shards(): gram = lax.psum(gram, 'tp')]
    all_gather x0 -> x1, waiting for transfers between devices: none -> 25.9 us  [shards(): gram = jnp.sum(lax.all_gather(gram, 'tp'), axis=0)]
    dot_general x15, matrix products: 9.65 us -> 7.57 us  [mul(): return jnp.einsum('mij,mjk->mik', a, b, precision=lax.Precision.HIGHEST)]
where the time goes in v1:
time: 169 us
  blocking collectives  107 us (63%)
  waiting for transfers between devices  25.9 us (15%)
  between operations  14.2 us (8%)
  matrix products  10.3 us (6%)
  other arithmetic  8.18 us (5%)
  local copies, waits for them, and re-layouts  3.17 us (2%)
    all_to_all x1, blocking collectives, shards(): lax.all_to_all(direction, 'fsdp', split_axis=0, concat_axis=1, tiled=True)  54.3 us
    all_to_all x1, blocking collectives, shards(): lax.all_to_all(iterate, 'fsdp', split_axis=1, concat_axis=0, tiled=True)  52.4 us
    all_gather x1, waiting for transfers between devices, shards(): gram = jnp.sum(lax.all_gather(gram, 'tp'), axis=0)  25.9 us
    dot_general x15, matrix products, mul(): return jnp.einsum('mij,mjk->mik', a, b, precision=lax.Precision.HIGHEST)  7.57 us
    add x1, other arithmetic, shards(): direction = hold_rate * new_momentum + gradients  4.27 us
  transfers between devices with their start and end apart: 1, of which 1 were waited for; matrix products, arithmetic and copies ran while one was open for 0% of the time, Pallas kernels for 0%

profile of v1, /device:TPU:0, one launch (start us, length us, event | category | flops | bytes accessed | tf_op | source)
XLA Modules:
  0.0 168.5 jit_solution(15080903002159324298)
XLA Ops:
  7.2 0.0 all-gather.3.cloned.1.call-start
  7.2 4.3 %multiply_add_fusion = (f32[16,32,1024]{2,1,0:T(8,128)S(1)}, f32[16,32,1024]{2,1,0:T(8,128)}) fusion(f32[16,32,1024]{2,1,0:T(8,128)} %param.3, f32[16,32,1024]{2,1,0:T(8,128)} %param.4), kind=kLoop, calls=%fused_computation.1 | loop fusion | flops 2097152 | bytes 8388608 | tf_op jit(solution)/shard_map/add | solution.py:31
  11.5 54.3 %all_to_all.27 = f32[16,32,1024]{2,1,0:T(8,128)S(1)} all-to-all(f32[16,32,1024]{2,1,0:T(8,128)S(1)} %get-tuple-element.2), channel_id=1, replica_groups=mesh['copy'=2,'fsdp'=4,'tp'=4] {'fsdp'}, dimensions={0} | all-to-all | bytes 4194304 | tf_op jit(solution)/shard_map/all_to_all | solution.py:32
  65.8 0.2 copy.7
  66.1 2.8 %fusion.13 = f32[4,128,128]{2,1,0:T(8,128)} fusion(f32[4,128,1024]{2,1,0:T(8,128)S(1)} %bitcast.38), kind=kOutput, calls=%fused_computation.25 | convolution fusion | flops 805306368 | bytes 2359296 | tf_op jit(solution)/shard_map/mik,mjk->mij/dot_general | solution.py:33
  68.8 0.0 all-gather.3.cloned.1.call-update
  68.9 25.9 %all-gather.3.cloned.1.call-done = f32[16,128,128]{2,1,0:T(8,128)} async-done(((f32[4,128,128]{2,1,0:T(8,128)}), f32[16,128,128]{2,1,0:T(8,128)}) %all-gather.3.cloned.1.call-update) | async-done | bytes 1048592 | tf_op jit(solution)/shard_map/all_gather | solution.py:34
  94.7 1.3 reduce_sum.18
  96.0 0.1 multiply_reduce_fusion
  96.2 0.5 fusion.3
  96.7 0.4 fusion.6
  97.1 0.4 fusion.4
  97.6 0.4 fusion.14
  98.0 0.4 fusion.2
  98.4 0.4 fusion.15
  98.8 0.4 fusion.19
  99.2 0.4 fusion.16
  99.6 0.4 fusion.1
  100.0 0.4 fusion.17
  100.4 0.4 fusion.20
  100.8 0.4 fusion.18
  101.2 0.4 fusion
  101.5 0.4 fusion.21
  101.9 1.9 %fusion.22 = f32[4,128,1024]{2,1,0:T(8,128)S(1)} fusion(f32[4,128,128]{2,1,0:T(8,128)S(1)} %fusion.21, f32[4,128,1024]{2,1,0:T(8,128)S(1)} %bitcast.39), kind=kOutput, calls=%fused_computation.34 | convolution fusion | flops 805306368 | bytes 4456448 | tf_op jit(solution)/shard_map/mij,mjk->mik/dot_general | solution.py:13
  103.9 1.4 copy.8
  105.2 52.4 %all_to_all.28 = f32[4,128,1024]{2,0,1:T(4,128)S(1)} all-to-all(f32[4,128,1024]{2,0,1:T(4,128)S(1)} %copy.8), channel_id=1, replica_groups=mesh['copy'=2,'fsdp'=4,'tp'=4] {'fsdp'}, dimensions={1} | all-to-all | bytes 4194304 | tf_op jit(solution)/shard_map/all_to_all | solution.py:36
  157.7 0.7 broadcast_multiply_fusion
  158.4 0.0 copy-start
  158.4 1.2 copy.9
  159.6 0.4 copy-done
  159.9 1.8 %bitcast_subtract_fusion = f32[16,32,1024]{2,1,0:T(8,128)} fusion(f32[4,4,32,1024]{3,2,1,0:T(8,128)S(1)} %copy.9, f32[16,32,1024]{2,1,0:T(8,128)S(1)} %copy-done), kind=kLoop, calls=%fused_computation | loop fusion | flops 1048576 | bytes 6291456 | tf_op jit(solution)/shard_map/sub | solution.py:37
  (3 shorter events, 0.0 us)
Async XLA Ops:
  7.2 87.6 %all-gather.3.cloned.1.call-start = ((), (), s32[]{:S(2)}) async-start(), calls=%async_computation.2 | async-start | bytes 1310720 | tf_op jit(solution)/shard_map/all_gather | solution.py:34
  158.4 1.6 copy-start
Sparse Core Ops, SparseCore 0:
  69.0 25.7 all-gather.2
